TPU v7x, 512 devices: a whole 4x8x8 slice. The times are simulated.
512 devices in a mesh: space: 128 (over z, y, core), ens: 4 (over x).
Axes of the slice: x: 4, y: 8, z: 8, core: 2. Of those that a mesh axis runs over, the one named last changes fastest.
Arguments:
- innovations: bfloat16 [4, 8192, 128, 128], P('ens', 'space'), may hold values from -6 to 6
- block_owner: int32 [8192, 1], P('space'), may hold values from 0 to 127; in each aligned block of 64 rows (0 to 63, 64 to 127, ...) at most 2 rows name the same one
- block_tile: int32 [8192], P('space'), may hold values from 0 to 3
- block_count: int32 [128], P('space'), may hold values from 48 to 64
- obs_row: int32 [8192, 128], P('space'), may hold values from 0 to 6
- obs_col: int32 [8192, 128], P('space'), may hold values from 0 to 14
- offsets: float32 [8192, 2, 128], P('space'), may hold values from 0 to 1
- obs_mask: int32 [8192, 128], P('space'), may hold values 0 or 1
- sigma: float32 [512, 128], P('space'), may hold values from 0.3 to 3
- coupling: float32 [128, 128], replicated, may hold values from -0.5 to 0.5
Outputs:
- gradient: float32 [128, 512, 128], P('ens', 'space')
Inputs may be any that keep to these rules, and one draw needn't show every extreme that they name: `block_owner`: among the rows of one device, no owner is named more than 2 times, and one owner is named exactly 2 times in some devices' rows. `block_count`: blocks of a device at positions at or above its count are padding.
All inputs are finite; a program needn't handle non-finite values. No bound on the sum of `obs_mask` on one device may be relied on, other than what follows from the above.
Results may differ from a plain program's by a relative error of at most 0.0095.
Values may be sent and summed in bfloat16 or wider, within the bound.
A program may use at most 64 MiB of HBM per device.

v0:
```python
import jax
import jax.numpy as jnp
from jax import lax
from jax.sharding import PartitionSpec as P

TW = 16


def in_blocks(x, dim, devices):
    shape = x.shape
    pieces = x.reshape(*shape[:dim], devices, shape[dim] // devices, *shape[dim + 1 :])
    return jnp.moveaxis(pieces, dim, 0)


def sent_and_summed(x, axis, dim):
    pieces = in_blocks(x, dim, lax.axis_size(axis))
    arrived = lax.all_to_all(pieces, axis, split_axis=0, concat_axis=0, tiled=True)
    return arrived.astype(jnp.float32).sum(axis=0)


def scaled_rows(totals, coupling, sigma, members):
    coupled = jnp.einsum("ck,tkh->cth", coupling, totals, precision=lax.Precision.HIGHEST)
    return sigma[None, :, :] * (jnp.transpose(totals, (1, 0, 2)) + coupled) / members


def accumulate_all(got_values, got_weights, got_places, tile_local, cell_count):
    group = 64
    width = got_values.shape[2]
    slot_total = got_values.shape[0]
    cell_ids = jnp.arange(cell_count, dtype=jnp.int32)
    tile_ids = jnp.arange(tile_local, dtype=jnp.int32)
    nothing = jnp.zeros((), got_values.dtype)

    def accumulate(turn, totals):
        start = turn * group
        values = lax.dynamic_slice_in_dim(got_values, start, group, 0)
        weights = lax.dynamic_slice_in_dim(got_weights, start, group, 0)
        places = lax.dynamic_slice_in_dim(got_places, start, group, 0).astype(jnp.int32)
        base = places[:, 0, :] * TW + places[:, 1, :]
        offset = cell_ids[None, :, None] - base[:, None, :]
        table = jnp.where(
            offset == 0,
            weights[:, 0, :][:, None, :],
            jnp.where(
                offset == 1,
                weights[:, 1, :][:, None, :],
                jnp.where(
                    offset == TW,
                    weights[:, 2, :][:, None, :],
                    jnp.where(offset == TW + 1, weights[:, 3, :][:, None, :], nothing),
                ),
            ),
        )
        contrib = jnp.einsum("gco,goh->gch", table, values, precision=lax.Precision.HIGHEST)
        pick = (tile_ids[:, None] == places[None, :, 2, 0]).astype(jnp.float32)
        return totals + jnp.einsum("tg,gch->tch", pick, contrib, precision=lax.Precision.HIGHEST)

    return lax.fori_loop(
        0, slot_total // group, accumulate, jnp.zeros((tile_local, cell_count, width), jnp.float32)
    )


def on_device(
    innovations,
    block_owner,
    block_tile,
    block_count,
    obs_row,
    obs_col,
    offsets,
    obs_mask,
    sigma,
    coupling,
):
    peers = lax.axis_size("space")
    blk_local = innovations.shape[1]
    obs_count = innovations.shape[2]
    width = innovations.shape[3]
    tile_local = sigma.shape[0]
    cell_count = coupling.shape[0]
    capacity = max(2, 2 * blk_local // peers)
    slot_total = peers * capacity
    position = jnp.arange(blk_local, dtype=jnp.int32)
    alive = (position < block_count[0]).astype(jnp.float32)
    live = obs_mask.astype(jnp.float32) * alive[:, None]
    row_frac = offsets[:, 0, :]
    col_frac = offsets[:, 1, :]
    corner_weights = jnp.stack(
        [
            (1.0 - row_frac) * (1.0 - col_frac),
            (1.0 - row_frac) * col_frac,
            row_frac * (1.0 - col_frac),
            row_frac * col_frac,
        ],
        axis=1,
    )
    corner_weights = (corner_weights * live[:, None, :]).astype(jnp.bfloat16)
    tile_rows = jnp.broadcast_to(block_tile[:, None], obs_row.shape)
    placing = jnp.stack([obs_row, obs_col, tile_rows], axis=1)
    owner = block_owner[:, 0]
    earlier = (owner[:, None] == owner[None, :]) & (position[None, :] < position[:, None])
    slot = owner * capacity + jnp.sum(earlier.astype(jnp.int32), axis=1)
    ens_count = lax.axis_size("ens")
    members = ens_count * innovations.shape[0]
    quarter = width // ens_count
    summed_innov = sent_and_summed(
        innovations[0].astype(jnp.float32).astype(jnp.bfloat16), "ens", 2
    )
    send_values = (
        jnp.zeros((slot_total, obs_count, quarter), jnp.float32).at[slot].set(summed_innov)
    )
    send_weights = (
        jnp.zeros((slot_total, 4, obs_count), jnp.float32)
        .at[slot]
        .set(corner_weights.astype(jnp.float32))
    )
    send_places = (
        jnp.zeros((slot_total, 3, obs_count), jnp.float32).at[slot].set(placing.astype(jnp.float32))
    )
    got_values, got_weights, got_places = (
        lax.all_to_all(
            send_values.astype(jnp.bfloat16), "space", split_axis=0, concat_axis=0, tiled=True
        ).astype(send_values.dtype),
        lax.all_to_all(
            send_weights.astype(jnp.bfloat16), "space", split_axis=0, concat_axis=0, tiled=True
        ).astype(send_weights.dtype),
        lax.all_to_all(
            send_places.astype(jnp.bfloat16), "space", split_axis=0, concat_axis=0, tiled=True
        ).astype(send_places.dtype),
    )
    totals = accumulate_all(got_values, got_weights, got_places, tile_local, cell_count)
    sigma_own = lax.dynamic_slice_in_dim(sigma, lax.axis_index("ens") * quarter, quarter, 1)
    scaled = scaled_rows(totals, coupling, sigma_own, members)
    return lax.all_to_all(
        scaled.astype(jnp.bfloat16), "ens", split_axis=0, concat_axis=2, tiled=True
    ).astype(scaled.dtype)


def solution(mesh):
    in_specs = (
        P("ens", "space", None, None),
        P("space", None),
        P("space"),
        P("space"),
        P("space", None),
        P("space", None),
        P("space", None, None),
        P("space", None),
        P("space", None),
        P(),
    )
    out_specs = P("ens", "space", None)
    return jax.shard_map(
        on_device, mesh=mesh, in_specs=in_specs, out_specs=out_specs, check_vma=False
    )
```

profile of v0, /device:TPU:1, one launch (start us, length us, event | category | flops | bytes accessed | tf_op | source)
XLA Modules:
  0.0 211.0 jit_solution(5730980256549630504)
XLA Ops:
  0.0 0.9 convert_reduce_fusion.1
  1.6 0.7 stack_broadcast_in_dim.2
  2.3 0.8 add_convert_fusion
  3.2 2.4 %scatter_fusion = f32[256,3,128]{2,1,0:T(4,128)S(1)} fusion(f32[256,3,128]{2,1,0:T(4,128)S(1)} %broadcast_in_dim.113, s32[64]{0:T(128)S(1)} %fusion.47, f32[64,3,128]{2,1,0:T(4,128)S(1)} %copy.51), kind=kCustom, calls=%fused_computation | custom fusion | bytes 295168 | tf_op jit(solution)/shard_map/scatter | solution.py:118
  5.7 0.8 convert_element_type.72
  6.5 18.4 %all-to-all-start = ((bf16[256,3,128]{2,1,0:T(4,128)(2,1)}), bf16[256,3,128]{2,1,0:T(4,128)(2,1)S(1)}, u32[]{:S(2)}, u32[]{:S(2)}) async-start(bf16[256,3,128]{2,1,0:T(4,128)(2,1)} %convert_element_type.72), calls=%async_computation | async-start | bytes 524288 | tf_op jit(solution)/shard_map/all_to_all | solution.py:127
  24.9 3.2 %copy.52 = bf16[1,64,128,128]{2,3,1,0:T(8,128)(2,1)S(1)} copy(bf16[1,64,128,128]{3,2,1,0:T(8,128)(2,1)} %param.12) | data formatting | bytes 4194304 | tf_op args[0]
  28.2 1.7 copy.53
  29.9 10.2 %all-to-all-done = bf16[256,3,128]{2,1,0:T(4,128)(2,1)S(1)} async-done(((bf16[256,3,128]{2,1,0:T(4,128)(2,1)}), bf16[256,3,128]{2,1,0:T(4,128)(2,1)S(1)}, u32[]{:S(2)}, u32[]{:S(2)}) %all-to-all-start) | async-done | bytes 196640 | tf_op jit(solution)/shard_map/all_to_all | solution.py:127
  40.1 4.0 %all-to-all-start.2 = ((bf16[4,64,128,32]{2,3,1,0:T(8,128)(2,1)}), bf16[4,64,128,32]{2,3,1,0:T(8,128)(2,1)S(1)}, u32[]{:S(2)}, u32[]{:S(2)}) async-start(bf16[4,64,128,32]{2,3,1,0:T(8,128)(2,1)} %copy.53), calls=%async_computation.2 | async-start | bytes 4194304 | tf_op jit(solution)/shard_map/all_to_all | solution.py:17
  45.2 2.4 %scatter_fusion.1 = f32[256,4,128]{2,1,0:T(4,128)S(1)} fusion(f32[256,4,128]{2,1,0:T(4,128)S(1)} %broadcast_in_dim.114, s32[64]{0:T(128)S(1)} %fusion.47, f32[64,4,128]{2,1,0:T(4,128)S(1)} %fusion.43), kind=kCustom, calls=%fused_computation.1 | custom fusion | bytes 393472 | tf_op jit(solution)/shard_map/scatter | solution.py:115
  47.7 0.8 convert_element_type.78
  48.5 21.5 %all-to-all-done.2 = bf16[4,64,128,32]{2,3,1,0:T(8,128)(2,1)S(1)} async-done(((bf16[4,64,128,32]{2,3,1,0:T(8,128)(2,1)}), bf16[4,64,128,32]{2,3,1,0:T(8,128)(2,1)S(1)}, u32[]{:S(2)}, u32[]{:S(2)}) %all-to-all-start.2) | async-done | bytes 2097184 | tf_op jit(solution)/shard_map/all_to_all | solution.py:17
  69.9 7.7 %all-to-all-start.1 = ((bf16[256,4,128]{2,1,0:T(4,128)(2,1)}), bf16[256,4,128]{2,1,0:T(4,128)(2,1)}, u32[]{:S(2)}, u32[]{:S(2)}) async-start(bf16[256,4,128]{2,1,0:T(4,128)(2,1)} %convert_element_type.78), calls=%async_computation.1 | async-start | bytes 524288 | tf_op jit(solution)/shard_map/all_to_all | solution.py:124
  78.0 2.5 %broadcast_in_dim.115 = f32[256,128,32]{1,2,0:T(8,128)} broadcast(f32[]{:T(128)} %constant.70.clone.1), dimensions={} | broadcast | bytes 4194308 | tf_op jit(solution)/shard_map/broadcast_in_dim | solution.py:110
  80.4 8.1 %scatter_fusion.2 = f32[256,128,32]{1,2,0:T(8,128)} fusion(f32[256,128,32]{1,2,0:T(8,128)} %broadcast_in_dim.115, s32[64]{0:T(128)S(1)} %fusion.47, f32[64,128,32]{1,2,0:T(8,128)S(1)} %convert_reduce_fusion), kind=kCustom, calls=%fused_computation.2 | custom fusion | bytes 3145984 | tf_op jit(solution)/shard_map/scatter | solution.py:110
  88.6 4.0 %convert_element_type.81 = bf16[256,128,32]{1,2,0:T(8,128)(2,1)} convert(f32[256,128,32]{1,2,0:T(8,128)} %scatter_fusion.2) | non-fusion elementwise | flops 1048576 | bytes 6291456 | tf_op jit(solution)/shard_map/convert_element_type | solution.py:122
  92.6 13.8 %all-to-all-start.3 = ((bf16[256,128,32]{1,2,0:T(8,128)(2,1)}), bf16[256,128,32]{1,2,0:T(8,128)(2,1)S(1)}, u32[]{:S(2)}, u32[]{:S(2)}) async-start(bf16[256,128,32]{1,2,0:T(8,128)(2,1)} %convert_element_type.81), calls=%async_computation.3 | async-start | bytes 4194304 | tf_op jit(solution)/shard_map/all_to_all | solution.py:121
  106.6 1.0 convert_element_type.79
  107.6 50.1 %all-to-all-done.3 = bf16[256,128,32]{1,2,0:T(8,128)(2,1)S(1)} async-done(((bf16[256,128,32]{1,2,0:T(8,128)(2,1)}), bf16[256,128,32]{1,2,0:T(8,128)(2,1)S(1)}, u32[]{:S(2)}, u32[]{:S(2)}) %all-to-all-start.3) | async-done | bytes 2097184 | tf_op jit(solution)/shard_map/all_to_all | solution.py:121
  157.7 2.5 %convert_element_type.82 = f32[256,128,32]{1,2,0:T(8,128)} convert(bf16[256,128,32]{1,2,0:T(8,128)(2,1)S(1)} %all-to-all-done.3) | non-fusion elementwise | flops 1048576 | bytes 6291456 | tf_op jit(solution)/shard_map/convert_element_type | solution.py:123
  160.2 42.3 %while.14 = (s32[]{:T(128)}, f32[4,128,32]{1,0,2:T(4,128)S(1)}, f32[256,3,128]{2,1,0:T(4,128)S(1)}, f32[256,4,128]{2,1,0:T(4,128)S(1)}, f32[256,128,32]{1,2,0:T(...) while((s32[]{:T(128)}, f32[4,128,32]{1,0,2:T(4,128)S(1)}, ...), condition=%wide.region_6.7_spmd.clone, body=%wide.region_5.6_spmd.clone.sunk | while | flops 424747264 | bytes 4457449 | solution.py:58
  160.7 9.0 %fusion.59 = f32[64,128,32]{1,2,0:T(8,128)S(1)} fusion(f32[64,128]{1,0:T(8,128)S(1)} %bitcast.70, f32[64,128]{1,0:T(8,128)S(1)} %bitcast.68, f32[64,128]{1,0:T(8,128)S(1)} %bitcast.69, f32[64,128]{1,0:T(8,128)S(1)} %bitcast.67, s32[64,128]{1,0:T(8,128)S(1)} %copy.75, f32[256,128,32]{1,2,0:T(8,128)} %get-tuple-element.262, s32[]{:T(128)S(6)} %select_n.81), kind=kOutput, calls=%fused_computation.10.clone.1 | convolution fusion | flops 412090368 | bytes 2260996 | tf_op jit(solution)/shard_map/while/body/eval_jaxpr/gco,goh->gch/dot_general | solution.py:54
  169.7 1.1 convolution_add_fusion.2
  171.2 9.0 %fusion.59 = f32[64,128,32]{1,2,0:T(8,128)S(1)} fusion(f32[64,128]{1,0:T(8,128)S(1)} %bitcast.70, f32[64,128]{1,0:T(8,128)S(1)} %bitcast.68, f32[64,128]{1,0:T(8,128)S(1)} %bitcast.69, f32[64,128]{1,0:T(8,128)S(1)} %bitcast.67, s32[64,128]{1,0:T(8,128)S(1)} %copy.75, f32[256,128,32]{1,2,0:T(8,128)} %get-tuple-element.262, s32[]{:T(128)S(6)} %select_n.81), kind=kOutput, calls=%fused_computation.10.clone.1 | convolution fusion | flops 412090368 | bytes 2260996 | tf_op jit(solution)/shard_map/while/body/eval_jaxpr/gco,goh->gch/dot_general | solution.py:54
  180.3 1.1 convolution_add_fusion.2
  181.8 9.0 %fusion.59 = f32[64,128,32]{1,2,0:T(8,128)S(1)} fusion(f32[64,128]{1,0:T(8,128)S(1)} %bitcast.70, f32[64,128]{1,0:T(8,128)S(1)} %bitcast.68, f32[64,128]{1,0:T(8,128)S(1)} %bitcast.69, f32[64,128]{1,0:T(8,128)S(1)} %bitcast.67, s32[64,128]{1,0:T(8,128)S(1)} %copy.75, f32[256,128,32]{1,2,0:T(8,128)} %get-tuple-element.262, s32[]{:T(128)S(6)} %select_n.81), kind=kOutput, calls=%fused_computation.10.clone.1 | convolution fusion | flops 412090368 | bytes 2260996 | tf_op jit(solution)/shard_map/while/body/eval_jaxpr/gco,goh->gch/dot_general | solution.py:54
  190.9 1.1 convolution_add_fusion.2
  192.4 9.0 %fusion.59 = f32[64,128,32]{1,2,0:T(8,128)S(1)} fusion(f32[64,128]{1,0:T(8,128)S(1)} %bitcast.70, f32[64,128]{1,0:T(8,128)S(1)} %bitcast.68, f32[64,128]{1,0:T(8,128)S(1)} %bitcast.69, f32[64,128]{1,0:T(8,128)S(1)} %bitcast.67, s32[64,128]{1,0:T(8,128)S(1)} %copy.75, f32[256,128,32]{1,2,0:T(8,128)} %get-tuple-element.262, s32[]{:T(128)S(6)} %select_n.81), kind=kOutput, calls=%fused_computation.10.clone.1 | convolution fusion | flops 412090368 | bytes 2260996 | tf_op jit(solution)/shard_map/while/body/eval_jaxpr/gco,goh->gch/dot_general | solution.py:54
  201.4 1.1 convolution_add_fusion.2
  203.2 6.7 %all_to_all.29 = bf16[4,2,2048]{2,1,0:T(2,128)(2,1)S(1)} all-to-all(bf16[4,2,2048]{2,1,0:T(2,128)(2,1)S(1)} %reshape.49), channel_id=1, replica_groups=mesh['space'=128,'ens'=4] {'ens'}, dimensions={0} | all-to-all | bytes 65536 | tf_op jit(solution)/shard_map/all_to_all | solution.py:134
  210.2 0.8 reshape.21
  (55 shorter events, 4.1 us)
Async XLA Ops:
  0.0 202.6 %copy-start = (f32[128,128]{1,0:T(8,128)S(1)}, f32[128,128]{1,0:T(8,128)}, u32[]{:S(2)}) copy-start(f32[128,128]{1,0:T(8,128)} %param.21) | copy-start | bytes 196612
  6.5 33.6 %all-to-all-start = ((bf16[256,3,128]{2,1,0:T(4,128)(2,1)}), bf16[256,3,128]{2,1,0:T(4,128)(2,1)S(1)}, u32[]{:S(2)}, u32[]{:S(2)}) async-start(bf16[256,3,128]{2,1,0:T(4,128)(2,1)} %convert_element_type.72), calls=%async_computation | async-start | bytes 524288 | tf_op jit(solution)/shard_map/all_to_all | solution.py:127
  28.1 16.7 %copy-start.2 = (s32[64,128]{1,0:T(8,128)S(1)}, s32[64,128]{1,0:T(8,128)}, u32[]{:S(2)}) copy-start(s32[64,128]{1,0:T(8,128)} %param.19) | copy-start | bytes 98308
  28.2 16.8 %copy-start.1 = (f32[64,2,128]{2,1,0:T(2,128)S(1)}, f32[64,2,128]{2,1,0:T(2,128)}, u32[]{:S(2)}) copy-start(f32[64,2,128]{2,1,0:T(2,128)} %param.18) | copy-start | bytes 196612
  40.1 29.8 %all-to-all-start.2 = ((bf16[4,64,128,32]{2,3,1,0:T(8,128)(2,1)}), bf16[4,64,128,32]{2,3,1,0:T(8,128)(2,1)S(1)}, u32[]{:S(2)}, u32[]{:S(2)}) async-start(bf16[4,64,128,32]{2,3,1,0:T(8,128)(2,1)} %copy.53), calls=%async_computation.2 | async-start | bytes 4194304 | tf_op jit(solution)/shard_map/all_to_all | solution.py:17
  69.9 22.7 %all-to-all-start.1 = ((bf16[256,4,128]{2,1,0:T(4,128)(2,1)}), bf16[256,4,128]{2,1,0:T(4,128)(2,1)}, u32[]{:S(2)}, u32[]{:S(2)}) async-start(bf16[256,4,128]{2,1,0:T(4,128)(2,1)} %convert_element_type.78), calls=%async_computation.1 | async-start | bytes 524288 | tf_op jit(solution)/shard_map/all_to_all | solution.py:124
  88.6 17.9 %copy-start.3 = (f32[4,128]{1,0:T(4,128)S(1)}, f32[4,128]{1,0:T(4,128)}, u32[]{:S(2)}) copy-start(f32[4,128]{1,0:T(4,128)} %param.20) | copy-start | bytes 6148
  92.6 65.1 %all-to-all-start.3 = ((bf16[256,128,32]{1,2,0:T(8,128)(2,1)}), bf16[256,128,32]{1,2,0:T(8,128)(2,1)S(1)}, u32[]{:S(2)}, u32[]{:S(2)}) async-start(bf16[256,128,32]{1,2,0:T(8,128)(2,1)} %convert_element_type.81), calls=%async_computation.3 | async-start | bytes 4194304 | tf_op jit(solution)/shard_map/all_to_all | solution.py:121
where the time goes:
time: 215 us; the launch traced here: 211 us
  waiting for transfers between devices  81.9 us (38%)
  starting transfers between devices  43.9 us (20%)
  matrix products  40.8 us (19%)
  local copies, waits for them, and re-layouts  24.3 us (11%)
  other arithmetic  12.3 us (6%)
  blocking collectives  6.65 us (3%)
    all_to_all x1, waiting for transfers between devices, on_device(): lax.all_to_all(send_values.astype(jnp.bfloat16), 'space', split_axis=0, c...  50.1 us
    dot_general x4, matrix products, accumulate(): jnp.einsum('gco,goh->gch', table, values, precision=lax.Precision.HIGHEST)  35.9 us
    all_to_all x1, waiting for transfers between devices, sent_and_summed(): lax.all_to_all(pieces, axis, split_axis=0, concat_axis=0, tiled=True)  21.5 us
    all_to_all x1, starting transfers between devices, on_device(): lax.all_to_all(send_places.astype(jnp.bfloat16), 'space', split_axis=0, c...  18.4 us
    all_to_all x1, starting transfers between devices, on_device(): lax.all_to_all(send_values.astype(jnp.bfloat16), 'space', split_axis=0, c...  13.8 us
    all_to_all x1, waiting for transfers between devices, on_device(): lax.all_to_all(send_places.astype(jnp.bfloat16), 'space', split_axis=0, c...  10.2 us
    scatter x1, local copies, waits for them, and re-layouts, on_device(): jnp.zeros((slot_total, obs_count, quarter), jnp.float32).at[slot]  8.12 us
    all_to_all x1, starting transfers between devices, on_device(): lax.all_to_all(send_weights.astype(jnp.bfloat16), 'space', split_axis=0,...  7.71 us
  transfers between devices with their start and end apart: 4, of which 4 were waited for; matrix products, arithmetic and copies ran while one was open for 12% of the time, Pallas kernels for 0%

commit v1 on v0

v1 whole, which is shorter than its diff:
```python
import jax
import jax.numpy as jnp
from jax import lax
from jax.experimental import pallas as pl
from jax.experimental.pallas import tpu as pltpu
from jax.sharding import PartitionSpec as P

MESH = pl.DeviceIdType.MESH
F32 = jnp.float32
BF16 = jnp.bfloat16
NX = 4
NR = 8
ROWS = 8
TW = 16
BLK = 64
CHUNK = 8
FAR = ((4, 3), (6, 1), (5, 2), (7, 0))


def kernel(
    key_ref,
    count_ref,
    inn_hbm,
    row_ref,
    col_ref,
    off_ref,
    mask_ref,
    sigma_ref,
    coup_ref,
    out_ref,
    inn,
    csend,
    fwd,
    comb,
    recv,
    other,
    vals,
    asend,
    arecv,
    fin,
    brecv,
    mean,
    gath,
    maps,
    mapo,
    smap,
    in_sem,
    fsend_sem,
    frecv_sem,
    nsend_sem,
    nrecv_sem,
    dsend_sem,
    drecv_sem,
    msend_sem,
    mrecv_sem,
    local_sem,
    asend_sem,
    arecv_sem,
    bsend_sem,
    brecv_sem,
    gsend_sem,
    grecv_sem,
):
    s = lax.axis_index("space")
    x = lax.axis_index("ens")
    c = lax.rem(s, 2)
    y = lax.rem(lax.div(s, 2), NR)
    z = lax.div(s, 2 * NR)
    chip = s - c
    a = y + c * (z - y)
    b = z + c * (y - z)
    stride_a = 2 + (2 * NR - 2) * c
    stride_b = 2 * NR - (2 * NR - 2) * c
    me = 2 * x + c

    def wrap(value, size):
        return lax.rem(value + 2 * size, size)

    def group_device(dx, dc):
        return {"space": chip + wrap(c + dc, 2), "ens": wrap(x + dx, NX)}

    def ring_device(da, db):
        return {"space": wrap(a + da, NR) * stride_a + wrap(b + db, NR) * stride_b + c, "ens": x}

    def load(ch):
        blocks = pl.ds(ch * CHUNK, CHUNK)
        return pltpu.make_async_copy(inn_hbm.at[blocks], inn.at[blocks], in_sem.at[ch])

    for j in range(8):
        load((j >> 1) + 4 * (j & 1)).start()

    barrier = pltpu.get_barrier_semaphore()
    partners = [group_device(dx, dc) for dx in range(NX) for dc in range(2) if (dx, dc) != (0, 0)]
    partners += [ring_device(1, 0), ring_device(-1, 0)]
    partners += [ring_device(0, r) for r in range(1, NR)]
    for partner in partners:
        pl.semaphore_signal(barrier, inc=1, device_id=partner, device_id_type=MESH)

    sub = lax.broadcasted_iota(jnp.int32, (8, 128), 0)
    lane = lax.broadcasted_iota(jnp.int32, (8, 128), 1)
    tile_ids = lax.rem(sub, 4) * 128 + lane

    def note(i, found):
        first, last = found
        hit = tile_ids == key_ref[i]
        return jnp.minimum(first, jnp.where(hit, i, BLK)), jnp.maximum(last, jnp.where(hit, i, -1))

    first, last = lax.fori_loop(
        0, BLK, note, (jnp.full((8, 128), BLK, jnp.int32), jnp.full((8, 128), -1, jnp.int32))
    )
    second = jnp.where((last == first) | (last < 0), BLK, last)
    maps[...] = jnp.where(sub < 4, first, second)
    for rel in range(2):
        vals[rel, BLK] = jnp.zeros((TW, 128), F32)

    def far_copy(par, i):
        sign = 1 - 2 * par
        blocks = pl.ds((4 * par + i) * CHUNK, CHUNK)
        return pltpu.make_async_remote_copy(
            src_ref=csend.at[pl.ds(2 * wrap(x + 2, NX), 2), blocks],
            dst_ref=fwd.at[par, i],
            send_sem=fsend_sem.at[par, i],
            recv_sem=frecv_sem.at[par, i],
            device_id={"space": s, "ens": wrap(x + sign, NX)},
            device_id_type=MESH,
        )

    def near_copy(slot, ch, rel, src):
        sign = 1 - 2 * slot
        return pltpu.make_async_remote_copy(
            src_ref=src,
            dst_ref=recv.at[slot, rel, pl.ds(ch * CHUNK, CHUNK)],
            send_sem=nsend_sem.at[slot, rel, ch],
            recv_sem=nrecv_sem.at[slot, rel, ch],
            device_id={"space": chip + wrap(c + rel, 2), "ens": wrap(x + sign, NX)},
            device_id_type=MESH,
        )

    def near_own(slot, ch, rel):
        sign = 1 - 2 * slot
        row = 2 * wrap(x + sign, NX) + wrap(c + rel, 2)
        return near_copy(slot, ch, rel, csend.at[row, pl.ds(ch * CHUNK, CHUNK)])

    def near_comb(par, i, rel):
        return near_copy(par, 4 * par + i, rel, comb.at[par, i, rel])

    def core_copy(ch):
        blocks = pl.ds(ch * CHUNK, CHUNK)
        return pltpu.make_async_remote_copy(
            src_ref=csend.at[2 * x + 1 - c, blocks],
            dst_ref=other.at[blocks],
            send_sem=dsend_sem.at[ch],
            recv_sem=drecv_sem.at[ch],
            device_id=group_device(0, 1),
            device_id_type=MESH,
        )

    def map_copy():
        return pltpu.make_async_remote_copy(
            src_ref=maps,
            dst_ref=mapo,
            send_sem=msend_sem,
            recv_sem=mrecv_sem,
            device_id=group_device(0, 1),
            device_id_type=MESH,
        )

    iota8 = lax.broadcasted_iota(jnp.int32, (ROWS, 128), 0)
    iota16 = lax.broadcasted_iota(jnp.int32, (TW, 128), 0)
    count = count_ref[0]

    def first_phase(j, carry):
        par = lax.rem(j, 2)
        i = lax.div(j, 2)
        ch = 4 * par + i
        start = pl.multiple_of(ch * CHUNK, CHUNK)
        load(ch).wait()
        rows = row_ref[pl.ds(start, CHUNK), :]
        cols = col_ref[pl.ds(start, CHUNK), :]
        masks = mask_ref[pl.ds(start, CHUNK), :]
        for k in range(CHUNK):
            block = start + k
            fracs = off_ref[block]
            fy, fx = fracs[0:1], fracs[1:2]
            alive = jnp.where(block < count, 1.0, 0.0).astype(F32)
            live = masks[k : k + 1].astype(F32) * alive
            down = iota8 - rows[k : k + 1]
            right = iota16 - cols[k : k + 1]
            row_part = jnp.where(down == 0, 1.0 - fy, jnp.where(down == 1, fy, 0.0)) * live
            col_part = jnp.where(right == 0, 1.0 - fx, jnp.where(right == 1, fx, 0.0))
            table = (row_part[:, None, :] * col_part[None, :, :]).astype(BF16)
            table = table.reshape(ROWS * TW, 128)
            done = jnp.dot(table, inn[block], preferred_element_type=F32).astype(BF16)
            for g in range(ROWS):
                csend[g, block] = done[g * TW : (g + 1) * TW]

        @pl.when(j == 0)
        def _():
            pl.semaphore_wait(barrier, len(partners))
            map_copy().start()

        far_copy(par, i).start()
        near_own(1 - par, ch, 0).start()
        near_own(1 - par, ch, 1).start()
        core_copy(ch).start()
        return carry

    lax.fori_loop(0, 8, first_phase, 0)

    def merge(j, carry):
        par = lax.rem(j, 2)
        i = lax.div(j, 2)
        sign = 1 - 2 * par
        far_copy(par, i).wait_recv()
        for rel in range(2):
            core = wrap(c + rel, 2)
            row = 2 * wrap(x + sign, NX) + core

            def add(k, inner):
                block = (4 * par + i) * CHUNK + k
                comb[par, i, rel, k] = (
                    fwd[par, i, core, k].astype(F32) + csend[row, block].astype(F32)
                ).astype(BF16)
                return inner

            lax.fori_loop(0, CHUNK, add, 0, unroll=True)
            near_comb(par, i, rel).start()
        return carry

    lax.fori_loop(0, 8, merge, 0)

    own_map = pltpu.make_async_copy(maps, smap.at[0], local_sem.at[0])
    own_map.start()
    map_copy().wait_recv()
    other_map = pltpu.make_async_copy(mapo, smap.at[1], local_sem.at[1])
    other_map.start()
    own_map.wait()
    other_map.wait()

    def sum_members(j, carry):
        ch = 4 * lax.rem(j, 2) + lax.div(j, 2)
        core_copy(ch).wait_recv()
        for slot in range(2):
            for rel in range(2):
                near_own(slot, ch, rel).wait_recv()

        def add(k, inner):
            block = ch * CHUNK + k
            vals[0, block] = (
                recv[0, 0, block].astype(F32)
                + recv[1, 0, block].astype(F32)
                + csend[me, block].astype(F32)
            )
            vals[1, block] = (
                recv[0, 1, block].astype(F32)
                + recv[1, 1, block].astype(F32)
                + other[block].astype(F32)
            )
            return inner

        lax.fori_loop(0, CHUNK, add, 0, unroll=True)
        return carry

    lax.fori_loop(0, 8, sum_members, 0)

    def own_sum(t):
        hi, lo = lax.div(t, 128), lax.rem(t, 128)
        return (
            vals[0, smap[0, hi, lo]]
            + vals[0, smap[0, 4 + hi, lo]]
            + vals[1, smap[1, hi, lo]]
            + vals[1, smap[1, 4 + hi, lo]]
        )

    def ring_copy(way, step, q):
        return pltpu.make_async_remote_copy(
            src_ref=asend.at[way, step, q],
            dst_ref=arecv.at[way, step, q],
            send_sem=asend_sem.at[way, step, q],
            recv_sem=arecv_sem.at[way, step, q],
            device_id=ring_device(1 - 2 * way, 0),
            device_id_type=MESH,
        )

    steps = NR // 2
    for step in range(steps):
        for place in range(4):
            if step == 0 and place < 2:
                continue
            for way in range(2):
                q = (place + 2 * (1 - way)) % 4
                got = step > 1 or (step == 1 and place >= 2)
                if got:
                    ring_copy(way, step - 1, q).wait_recv()
                to_a = wrap(a + (1 - 2 * way) * (steps - step), NR)
                for half in range(2):
                    to_b = wrap(b + FAR[q][half], NR)
                    base = 4 * (to_a * stride_a + to_b * stride_b)

                    def add(k, inner):
                        total = own_sum(base + k)
                        if got:
                            total = total + arecv[way, step - 1, q, half * 8 + k].astype(F32)
                        asend[way, step, q, half * 8 + k] = total.astype(BF16)
                        return inner

                    lax.fori_loop(0, 8, add, 0, unroll=True)
                ring_copy(way, step, q).start()

    def line_copy(r):
        return pltpu.make_async_remote_copy(
            src_ref=fin.at[r],
            dst_ref=brecv.at[r],
            send_sem=bsend_sem.at[r],
            recv_sem=brecv_sem.at[r],
            device_id=ring_device(0, r),
            device_id_type=MESH,
        )

    for q in (0, 2, 1, 3):
        ring_copy(0, steps - 1, q).wait_recv()
        ring_copy(1, steps - 1, q).wait_recv()
        for half in range(2):
            r = FAR[q][half]
            base = 4 * (a * stride_a + wrap(b + r, NR) * stride_b)

            def add(k, inner):
                total = own_sum(base + k)
                for way in range(2):
                    total = total + arecv[way, steps - 1, q, half * 8 + k].astype(F32)
                if r == 0:
                    mean[k] = total
                else:
                    fin[r, k] = total.astype(BF16)
                return inner

            lax.fori_loop(0, 8, add, 0, unroll=True)
            if r != 0:
                line_copy(r).start()

    for r in range(1, NR):
        line_copy(r).wait_recv()

    def finish(k, carry):
        total = mean[k]
        for r in range(1, NR):
            total = total + brecv[r, k].astype(F32)
        fin[0, k] = total.astype(BF16)
        return carry

    lax.fori_loop(0, 8, finish, 0, unroll=True)

    def gather_copy(dx, dc):
        core = wrap(c + dc, 2)
        return pltpu.make_async_remote_copy(
            src_ref=fin.at[0, pl.ds(4 * core, 4)],
            dst_ref=gath.at[me],
            send_sem=gsend_sem.at[2 * dx + dc],
            recv_sem=grecv_sem.at[2 * dx + dc],
            device_id=group_device(dx, dc),
            device_id_type=MESH,
        )

    others = [(2, 0), (2, 1), (1, 0), (1, 1), (3, 0), (3, 1), (0, 1)]
    for dx, dc in others:
        gather_copy(dx, dc).start()
    for t in range(4):
        gath[me, t] = fin[0, 4 * c + t]

    def sent(j, carry):
        par = lax.rem(j, 2)
        i = lax.div(j, 2)
        far_copy(par, i).wait_send()
        core_copy(j).wait_send()
        for rel in range(2):
            near_own(0, j, rel).wait_send()
            near_own(1, j, rel).wait_send()
        return carry

    lax.fori_loop(0, 8, sent, 0)
    map_copy().wait_send()
    for step in range(steps):
        for place in range(4):
            if step == 0 and place < 2:
                continue
            for way in range(2):
                ring_copy(way, step, (place + 2 * (1 - way)) % 4).wait_send()
    for r in range(1, NR):
        line_copy(r).wait_send()

    coup = coup_ref[pl.ds(pl.multiple_of(32 * x, 32), 32), :]
    coup_hi = coup.astype(BF16)
    coup_lo = (coup - coup_hi.astype(F32)).astype(BF16)
    for dx, dc in others:
        gather_copy(dx, dc).wait_recv()
    for t in range(4):
        field = jnp.concatenate([gath[g, t] for g in range(ROWS)], axis=0)
        own = jnp.concatenate([gath[2 * x, t], gath[2 * x + 1, t]], axis=0).astype(F32)
        coupled = jnp.dot(coup_hi, field, preferred_element_type=F32)
        coupled = coupled + jnp.dot(coup_lo, field, preferred_element_type=F32)
        scaled = (own + coupled) * (sigma_ref[t : t + 1, :] * (1.0 / NX))
        out_ref[:, t, :] = scaled
    for dx, dc in others:
        gather_copy(dx, dc).wait_send()


def on_device(
    innovations,
    block_owner,
    block_tile,
    block_count,
    obs_row,
    obs_col,
    offsets,
    obs_mask,
    sigma,
    coupling,
):
    key = block_owner[:, 0] * 4 + block_tile
    vmem = pl.BlockSpec(memory_space=pltpu.VMEM)
    smem = pl.BlockSpec(memory_space=pltpu.SMEM)
    dma = pltpu.SemaphoreType.DMA
    tile = (TW, 128)
    return pl.pallas_call(
        kernel,
        out_shape=jax.ShapeDtypeStruct((32, 4, 128), F32),
        in_specs=[smem, smem, pl.BlockSpec(memory_space=pltpu.HBM)] + [vmem] * 6,
        out_specs=vmem,
        scratch_shapes=[
            pltpu.VMEM((BLK, 128, 128), BF16),
            pltpu.VMEM((ROWS, BLK) + tile, BF16),
            pltpu.VMEM((2, 4, 2, CHUNK) + tile, BF16),
            pltpu.VMEM((2, 4, 2, CHUNK) + tile, BF16),
            pltpu.VMEM((2, 2, BLK) + tile, BF16),
            pltpu.VMEM((BLK,) + tile, BF16),
            pltpu.VMEM((2, BLK + 1) + tile, F32),
            pltpu.VMEM((2, 4, 4, 16) + tile, BF16),
            pltpu.VMEM((2, 4, 4, 16) + tile, BF16),
            pltpu.VMEM((NR, 8) + tile, BF16),
            pltpu.VMEM((NR, 8) + tile, BF16),
            pltpu.VMEM((8,) + tile, F32),
            pltpu.VMEM((ROWS, 4) + tile, BF16),
            pltpu.VMEM((8, 128), jnp.int32),
            pltpu.VMEM((8, 128), jnp.int32),
            pltpu.SMEM((2, 8, 128), jnp.int32),
            dma((8,)),
            dma((2, 4)),
            dma((2, 4)),
            dma((2, 2, 8)),
            dma((2, 2, 8)),
            dma((8,)),
            dma((8,)),
            dma,
            dma,
            dma((2,)),
            dma((2, 4, 4)),
            dma((2, 4, 4)),
            dma((NR,)),
            dma((NR,)),
            dma((8,)),
            dma((8,)),
        ],
        compiler_params=pltpu.CompilerParams(
            collective_id=0, has_side_effects=True, vmem_limit_bytes=48 * 1024 * 1024
        ),
        name="adjoint",
    )(
        key,
        block_count,
        innovations[0],
        obs_row,
        obs_col,
        offsets,
        obs_mask,
        sigma,
        coupling,
    )


def solution(mesh):
    in_specs = (
        P("ens", "space", None, None),
        P("space", None),
        P("space"),
        P("space"),
        P("space", None),
        P("space", None),
        P("space", None, None),
        P("space", None),
        P("space", None),
        P(),
    )
    return jax.shard_map(
        on_device,
        mesh=mesh,
        in_specs=in_specs,
        out_specs=P("ens", "space", None),
        check_vma=False,
    )
```

time: 215 us -> 70.6 us (0.33); the launches traced: 211 us -> 70.1 us
  waiting for transfers between devices: 81.9 us -> 0 us
  Pallas kernels: 0 us -> 61.9 us
  starting transfers between devices: 43.9 us -> 0 us
  matrix products: 40.8 us -> 0 us
  local copies, waits for them, and re-layouts: 24.3 us -> 6.85 us
  other arithmetic: 12.3 us -> 0.68 us
  blocking collectives: 6.65 us -> 0 us
    all_to_all x4 -> x0, waiting for transfers between devices: 81.9 us -> none  [the longest x1 50.1 us: on_device(): lax.all_to_all(send_values.astype(jnp.bfloat16), 'space', split_axis=0, c...]
    pallas_call x0 -> x1, Pallas kernels: none -> 61.9 us  [on_device(): pl.pallas_call(kernel, out_shape=jax.ShapeDtypeStruct((32, 4, 128), F32),...]
    all_to_all x4 -> x0, starting transfers between devices: 43.9 us -> none  [the longest x1 18.4 us: on_device(): lax.all_to_all(send_places.astype(jnp.bfloat16), 'space', split_axis=0, c...]
    dot_general x9 -> x0, matrix products: 40.8 us -> none  [the longest x4 35.9 us: accumulate(): jnp.einsum('gco,goh->gch', table, values, precision=lax.Precision.HIGHEST)]
    scatter x3 -> x0, local copies, waits for them, and re-layouts: 13 us -> none  [the longest x1 8.12 us: on_device(): jnp.zeros((slot_total, obs_count, quarter), jnp.float32).at[slot]]
    convert_element_type x14 -> x0, other arithmetic: 10.2 us -> none  [the longest x1 4 us: on_device(): send_values.astype(jnp.bfloat16)]
    all_to_all x1 -> x0, blocking collectives: 6.65 us -> none  [on_device(): lax.all_to_all(scaled.astype(jnp.bfloat16), 'ens', split_axis=0, concat_a...]
    unnamed x11 -> x15, local copies, waits for them, and re-layouts: 3.54 us -> 6.85 us
  transfers between devices with their start and end apart: 4 -> 0, of which waited for: 4 -> 0; matrix products, arithmetic and copies ran while one was open for 12% -> 0% of each run, Pallas kernels for 0% -> 0%
where the time goes in v1:
time: 70.6 us; the launch traced here: 70.1 us
  Pallas kernels  61.9 us (88%)
  local copies, waits for them, and re-layouts  6.85 us (10%)
    pallas_call x1, Pallas kernels, on_device(): pl.pallas_call(kernel, out_shape=jax.ShapeDtypeStruct((32, 4, 128), F32),...  61.9 us
    unnamed x15, local copies, waits for them, and re-layouts  6.85 us

profile of v1, /device:TPU:1, one launch (start us, length us, event | category | flops | bytes accessed | tf_op | source)
XLA Modules:
  0.0 70.1 jit_solution(13131521269836067320)
XLA Ops:
  0.7 0.7 bitcast_add_fusion.key_ref
  1.3 0.0 copy-start
  1.3 1.6 %copy-done = bf16[1,64,128,128]{3,2,1,0:T(8,128)(2,1)S(1)} copy-done((bf16[1,64,128,128]{3,2,1,0:T(8,128)(2,1)S(1)}, bf16[1,64,128,128]{3,2,1,0:T(8,128)(2,1)}, u32[]{:S(2)}) %copy-start) | copy-done | bytes 2097176
  2.9 0.0 copy-start.1
  2.9 0.8 %copy-done.1 = f32[64,2,128]{2,1,0:T(2,128)S(1)} copy-done((f32[64,2,128]{2,1,0:T(2,128)S(1)}, f32[64,2,128]{2,1,0:T(2,128)}, u32[]{:S(2)}) %copy-start.1) | copy-done | bytes 65560
  3.8 0.0 copy-start.2
  3.8 0.8 %copy-done.2 = f32[128,128]{1,0:T(8,128)S(1)} copy-done((f32[128,128]{1,0:T(8,128)S(1)}, f32[128,128]{1,0:T(8,128)}, u32[]{:S(2)}) %copy-start.2) | copy-done | bytes 65560
  4.6 0.0 copy-start.3
  4.6 0.8 %copy-done.3 = s32[64,128]{1,0:T(8,128)S(1)} copy-done((s32[64,128]{1,0:T(8,128)S(1)}, s32[64,128]{1,0:T(8,128)}, u32[]{:S(2)}) %copy-start.3) | copy-done | bytes 32792
  5.4 0.0 copy-start.4
  5.4 0.8 %copy-done.4 = s32[64,128]{1,0:T(8,128)S(1)} copy-done((s32[64,128]{1,0:T(8,128)S(1)}, s32[64,128]{1,0:T(8,128)}, u32[]{:S(2)}) %copy-start.4) | copy-done | bytes 32792
  6.1 0.0 copy-start.5
  6.1 0.8 %copy-done.5 = s32[64,128]{1,0:T(8,128)S(1)} copy-done((s32[64,128]{1,0:T(8,128)S(1)}, s32[64,128]{1,0:T(8,128)}, u32[]{:S(2)}) %copy-start.5) | copy-done | bytes 32792
  6.9 0.0 copy-start.6
  6.9 0.7 copy-done.6
  7.6 61.9 %adjoint.1 = f32[32,4,128]{2,1,0:T(4,128)S(1)} custom-call(s32[64]{0:T(128)S(1)} %bitcast_add_fusion.key_ref, s32[1]{0:T(128)S(6)} %copy.12.count_ref, bf16[64,128,128]{2,1,0:T(8,128)(2,1)S(1)} %bitcast.3, s32[64,128]{1,0:T(8,128)S(1)} %copy-done.3, s32[64,128]{1,0:T(8,128)S(1)} %copy-done.4, f32[64,2,128]{2,1,0:T(2,128)S(1)} %copy-done.1, ...), custom_call_target="tpu_custom_call" | custom-call | tf_op jit(solution)/shard_map/adjoint/pallas_call | solution.py:424
  69.5 0.6 copy.13
Async XLA Ops:
  1.3 1.6 %copy-start = (bf16[1,64,128,128]{3,2,1,0:T(8,128)(2,1)S(1)}, bf16[1,64,128,128]{3,2,1,0:T(8,128)(2,1)}, u32[]{:S(2)}) copy-start(bf16[1,64,128,128]{3,2,1,0:T(8,128)(2,1)} %param.10) | copy-start | bytes 6291460
  2.9 0.8 %copy-start.1 = (f32[64,2,128]{2,1,0:T(2,128)S(1)}, f32[64,2,128]{2,1,0:T(2,128)}, u32[]{:S(2)}) copy-start(f32[64,2,128]{2,1,0:T(2,128)} %off_ref.1) | copy-start | bytes 196612
  3.8 0.8 %copy-start.2 = (f32[128,128]{1,0:T(8,128)S(1)}, f32[128,128]{1,0:T(8,128)}, u32[]{:S(2)}) copy-start(f32[128,128]{1,0:T(8,128)} %coup_ref.1) | copy-start | bytes 196612
  4.6 0.8 %copy-start.3 = (s32[64,128]{1,0:T(8,128)S(1)}, s32[64,128]{1,0:T(8,128)}, u32[]{:S(2)}) copy-start(s32[64,128]{1,0:T(8,128)} %row_ref.1) | copy-start | bytes 98308
  5.4 0.8 %copy-start.4 = (s32[64,128]{1,0:T(8,128)S(1)}, s32[64,128]{1,0:T(8,128)}, u32[]{:S(2)}) copy-start(s32[64,128]{1,0:T(8,128)} %col_ref.1) | copy-start | bytes 98308
  6.1 0.8 %copy-start.5 = (s32[64,128]{1,0:T(8,128)S(1)}, s32[64,128]{1,0:T(8,128)}, u32[]{:S(2)}) copy-start(s32[64,128]{1,0:T(8,128)} %mask_ref.1) | copy-start | bytes 98308
  6.9 0.7 copy-start.6
